TPU v7x, 32 devices: a whole 2x2x4 slice. The times are simulated.
32 devices in a mesh: band: 8 (over z, y), dom: 4 (over x, core).
Axes of the slice: x: 2, y: 2, z: 4, core: 2. Of those that a mesh axis runs over, the one named last changes fastest.
Arguments:
- wavefunctions: float32 [1024, 16, 16, 128], P('band', 'dom'), may hold values from -6 to 6
- potential: float32 [16, 16, 128], P('dom'), may hold values from -40 to 40
- projectors: float32 [16, 18, 4, 16, 128], P('dom'), may hold values from -0.0625 to 0.0625
- hamiltonian_correction: float32 [16, 18, 18], P('dom'), may hold values from -0.078125 to 0.078125
- delta_s: float32 [16, 18, 18], P('dom'), may hold values from -0.078125 to 0.078125
- projector_count: int32 [16], P('dom'), may hold values from 1 to 18
Outputs:
- ham: float32 [1024, 1024], P('band')
- correlation: float32 [1024, 1024], P('band')
All inputs are finite; a program needn't handle non-finite values.
Results may differ from a plain program's by a relative error of at most 0.00007.
Values sent between devices are 32-bit elements; how exact they have to be, the bound alone decides.
A program may use at most 192 MiB of HBM per device.

v0:
```python
import jax
import jax.numpy as jnp
from jax import lax
from jax.sharding import PartitionSpec as P


def with_halo(cells, sides, width):
    for axis, dim in sides:
        count = lax.axis_size(axis)
        head = lax.slice_in_dim(cells, 0, width, axis=dim)
        tail = lax.slice_in_dim(cells, cells.shape[dim] - width, cells.shape[dim], axis=dim)
        cells = jnp.concatenate(
            [
                lax.ppermute(tail, axis, [(i, (i + 1) % count) for i in range(count)]),
                cells,
                lax.ppermute(head, axis, [((i + 1) % count, i) for i in range(count)]),
            ],
            axis=dim,
        )
    return cells


def shifted(value, axis, steps):
    count = lax.axis_size(axis)
    pairs = [(source, (source + steps) % count) for source in range(count)]
    return lax.ppermute(value, axis, pairs)


def rows_product(left, right):
    return lax.dot_general(
        left,
        right,
        (((1,), (1,)), ((), ())),
        precision=lax.Precision.HIGHEST,
        preferred_element_type=jnp.float32,
    )


def kinetic_apply(padded, wavefn, potential):
    beside = padded[:, 2:] + padded[:, :-2]
    beside = beside + jnp.roll(wavefn, 1, 2) + jnp.roll(wavefn, -1, 2)
    beside = beside + jnp.roll(wavefn, 1, 3) + jnp.roll(wavefn, -1, 3)
    return 0.5 * (6.0 * wavefn - beside) + potential[None] * wavefn


def coefficients(flat_part, projector_flattened, slot_mask):
    return rows_product(flat_part, projector_flattened) * slot_mask[None, :]


def pair_blocks(own, piece_flat, piece_coef):
    hpsi_flat, psi_flat, coupled_h, coupled_s, volume = own
    ham_block = volume * rows_product(hpsi_flat, piece_flat) + rows_product(coupled_h, piece_coef)
    ovl_block = volume * rows_product(psi_flat, piece_flat) + rows_product(coupled_s, piece_coef)
    return (ham_block, ovl_block)


def place_blocks(carry, blocks, start):
    ham_rows = lax.dynamic_update_slice_in_dim(carry[0], blocks[0], start, 1)
    ovl_rows = lax.dynamic_update_slice_in_dim(carry[1], blocks[1], start, 1)
    return (ham_rows, ovl_rows)


def on_device(
    wavefunctions, potential, projectors, hamiltonian_correction, delta_s, projector_count
):
    band_count, cx, ny, nz = wavefunctions.shape
    groups = lax.axis_size("band")
    mine = lax.axis_index("band")
    grid_cells = cx * ny * nz
    volume = 1.0 / (grid_cells * lax.axis_size("dom"))
    padded = with_halo(wavefunctions, (("dom", 1),), 1)
    hpsi = kinetic_apply(padded, wavefunctions, potential)
    psi_flat = wavefunctions.reshape(band_count, grid_cells)
    hpsi_flat = hpsi.reshape(band_count, grid_cells)
    atom_list = hamiltonian_correction.shape[0]
    slot_count = hamiltonian_correction.shape[1]
    slot_mask = (
        (jnp.arange(slot_count, dtype=jnp.int32)[None, :] < projector_count[:, None])
        .astype(jnp.float32)
        .reshape(-1)
    )
    projector_flattened = projectors.reshape(atom_list * slot_count, grid_cells)
    projector_coefficient = coefficients(psi_flat, projector_flattened, slot_mask)
    sym_h = 0.5 * (hamiltonian_correction + jnp.swapaxes(hamiltonian_correction, 1, 2))
    sym_s = 0.5 * (delta_s + jnp.swapaxes(delta_s, 1, 2))
    coefficient_triple = projector_coefficient.reshape(band_count, atom_list, slot_count)
    coupled_h = jnp.einsum(
        "bap,apq->baq", coefficient_triple, sym_h, precision=lax.Precision.HIGHEST
    ).reshape(band_count, -1)
    coupled_s = jnp.einsum(
        "bap,apq->baq", coefficient_triple, sym_s, precision=lax.Precision.HIGHEST
    ).reshape(band_count, -1)
    own = (hpsi_flat, psi_flat, coupled_h, coupled_s, volume)
    total = band_count * groups
    empty = jnp.zeros((band_count, total), jnp.float32)
    half = groups // 2
    first = pair_blocks(own, psi_flat, projector_coefficient)
    started = place_blocks((empty, empty), first, mine * band_count)

    def step_with(step, state):
        moving, ham_rows, ovl_rows = state
        moving = shifted((moving[0], moving[1]), "band", 1)
        source = (mine - step) % groups
        blocks = pair_blocks(own, moving[0].reshape(band_count, grid_cells), moving[1])
        ham_rows, ovl_rows = place_blocks((ham_rows, ovl_rows), blocks, source * band_count)
        return (moving, ham_rows, ovl_rows)

    final = lax.fori_loop(
        1, half + 1, step_with, ((wavefunctions, projector_coefficient), started[0], started[1])
    )
    summed = (final[1], final[2])
    reduced = lax.psum((summed[0], summed[1]), "dom")
    ham_three = reduced[0].reshape(band_count, groups, band_count)
    ovl_three = reduced[1].reshape(band_count, groups, band_count)
    mirrored = (
        lax.all_to_all(ham_three, "band", split_axis=1, concat_axis=1, tiled=True),
        lax.all_to_all(ovl_three, "band", split_axis=1, concat_axis=1, tiled=True),
    )
    distance = (jnp.arange(groups, dtype=jnp.int32) - mine) % groups
    borrowed = ((distance >= 1) & (distance <= half - 1))[None, :, None]
    ham = jnp.where(borrowed, jnp.transpose(mirrored[0], (2, 1, 0)), ham_three).reshape(
        band_count, total
    )
    correlation = jnp.where(borrowed, jnp.transpose(mirrored[1], (2, 1, 0)), ovl_three).reshape(
        band_count, total
    )
    return (ham, correlation)


def solution(mesh):
    placed = (
        P("band", "dom", None, None),
        P("dom", None, None),
        P("dom", None, None, None, None),
        P("dom", None, None),
        P("dom", None, None),
        P("dom"),
    )
    return jax.shard_map(
        on_device,
        mesh=mesh,
        in_specs=placed,
        out_specs=(P("band", None), P("band", None)),
        check_vma=False,
    )
```

profile of v0, /device:TPU:0, one launch (start us, length us, event | category | flops | bytes accessed | tf_op | source)
XLA Modules:
  0.0 656.2 jit_solution(10761761207809537876)
XLA Ops:
  13.3 4.6 fusion.70
  18.4 8.2 %fusion.61 = f32[128,128]{1,0:T(8,128)S(1)} fusion(f32[128,4,16,128]{3,2,1,0:T(8,128)S(1)} %copy.150), kind=kOutput, calls=%fused_computation.36 | convolution fusion | flops 1610629120 | bytes 4259840 | tf_op jit(solution)/shard_map/dot_general | solution.py:30
  26.6 12.6 %reshape.82 = f32[72,8192]{1,0:T(8,128)S(1)} reshape(f32[4,18,4,16,128]{4,3,2,1,0:T(8,128)} %param.10) | data formatting | bytes 4718592 | tf_op jit(solution)/shard_map/reshape | solution.py:82
  39.4 8.6 %convolution_multiply_fusion = f32[128,72]{0,1:T(8,128)S(1)} fusion(f32[72,8192]{1,0:T(8,128)S(1)} %reshape.82, f32[72]{0:T(128)S(1)} %reshape.91, f32[16,8,64,128]{3,2,1,0:T(8,128)} %bitcast.105), kind=kOutput, calls=%fused_computation.39 | convolution fusion | flops 905978880 | bytes 6590752 | tf_op jit(solution)/shard_map/dot_general | solution.py:30
  48.9 7.4 %copy.123 = f32[16,8,64,128]{3,1,2,0:T(8,128)} copy(f32[16,8,64,128]{3,2,1,0:T(8,128)} %bitcast.106) | data formatting | bytes 8388608
  57.3 8.1 %fusion.71 = (f32[128,4,16,1]{3,2,1,0:T(8,128)}, f32[128,4,16,1]{3,2,1,0:T(8,128)}) fusion(f32[128,4,16,128]{3,2,1,0:T(8,128)} %copy-done), kind=kLoop, calls=%fused_computation.56 | loop fusion | bytes 131072 | tf_op jit(solution)/shard_map/jit(_roll_static)/slice | solution.py:42
  65.4 4.3 fusion.72
  69.7 11.5 %fusion.31 = f32[128,4,16,128]{3,2,1,0:T(8,128)S(1)} fusion(f32[128,4,16,128]{3,2,1,0:T(8,128)S(1)} %copy-done.1, f32[128,1,16,128]{3,2,1,0:T(8,128)} %collective-permute-done.3, f32[128,1,16,128]{3,2,1,0:T(8,128)} %collective-permute-done.2, f32[128,4,15,128]{3,2,1,0:T(8,128)} %get-tuple-element.317, f32[128,4,1,128]{3,2,1,0:T(1,128)S(1)} %get-tuple-element.319, ...), kind=kLoop, calls=%fused_computation.22 | loop fusion | flops 16777216 | bytes 27295744 | tf_op jit(solution)/shard_map/add | solution.py:43
  81.2 5.3 copy.122
  86.5 8.4 %fusion.56 = f32[128,1024]{1,0:T(8,128)S(1)} fusion(f32[128,1024]{1,0:T(8,128)S(1)} %broadcast_in_dim.19.clone, s32[]{:T(128)S(6)} %select_n.53, f32[128,128]{1,0:T(8,128)S(1)} %fusion.77, f32[128,4,16,128]{3,2,1,0:T(8,128)S(1)} %copy-done.1, f32[128,4,16,128]{3,2,1,0:T(8,128)S(1)} %fusion.31), kind=kOutput, calls=%fused_computation.35 | convolution fusion | flops 1610645504 | bytes 8519684 | tf_op jit(solution)/shard_map/dot_general | solution.py:30
  94.8 476.8 %while.21 = (s32[]{:T(128)}, f32[128,4,16,128]{3,2,1,0:T(8,128)}, f32[128,72]{1,0:T(8,128)S(1)}, f32[128,1024]{1,0:T(8,128)S(1)}, f32[128,1024]{1,0:T(8,128)S(1)...) while((s32[]{:T(128)}, f32[128,4,16,128]{3,2,1,0:T(8,128)}, ...), condition=%wide.region_1.2_spmd, body=%wide.region_0.1_spmd.sunk | while | flops 3249602560 | bytes 59482536 | solution.py:108
  98.0 94.5 %collective-permute-done.1 = f32[128,72]{1,0:T(8,128)S(1)} collective-permute-done((f32[128,72]{1,0:T(8,128)S(1)}, f32[128,72]{1,0:T(8,128)S(1)}, u32[]{:S(2)}, u32[]{:S(2)}) %collective-permute-start.1) | collective-permute-done | bytes 36896 | tf_op jit(solution)/shard_map/while/body/eval_jaxpr/ppermute | solution.py:26
  193.1 9.2 %fusion.112 = f32[128,1024]{1,0:T(8,128)S(1)} fusion(f32[128,1024]{1,0:T(8,128)S(1)} %get-tuple-element.404, s32[]{:T(128)S(6)} %select_n.64, f32[128,128]{1,0:T(8,128)S(1)} %fusion.111, f32[128,8192]{1,0:T(8,128)} %get-tuple-element.422, f32[16,8,64,128]{3,2,1,0:T(8,128)} %bitcast.104), kind=kOutput, calls=%fused_computation.8.clone.1 | convolution fusion | flops 1610645504 | bytes 8519684 | tf_op jit(solution)/shard_map/while/body/eval_jaxpr/dot_general | solution.py:30
  202.2 8.3 %fusion.114 = f32[128,1024]{1,0:T(8,128)S(1)} fusion(f32[128,1024]{1,0:T(8,128)S(1)} %get-tuple-element.405, s32[]{:T(128)S(6)} %select_n.64, f32[128,128]{1,0:T(8,128)S(1)} %fusion.113, f32[128,8192]{1,0:T(8,128)S(1)} %copy-done.2, f32[16,8,64,128]{3,2,1,0:T(8,128)} %bitcast.104), kind=kOutput, calls=%fused_computation.11.clone.1 | convolution fusion | flops 1610645504 | bytes 8519684 | tf_op jit(solution)/shard_map/while/body/eval_jaxpr/dot_general | solution.py:30
  210.5 4.8 copy.143
  216.4 95.6 %collective-permute-done.1 = f32[128,72]{1,0:T(8,128)S(1)} collective-permute-done((f32[128,72]{1,0:T(8,128)S(1)}, f32[128,72]{1,0:T(8,128)S(1)}, u32[]{:S(2)}, u32[]{:S(2)}) %collective-permute-start.1) | collective-permute-done | bytes 36896 | tf_op jit(solution)/shard_map/while/body/eval_jaxpr/ppermute | solution.py:26
  312.6 9.2 %fusion.112 = f32[128,1024]{1,0:T(8,128)S(1)} fusion(f32[128,1024]{1,0:T(8,128)S(1)} %get-tuple-element.404, s32[]{:T(128)S(6)} %select_n.64, f32[128,128]{1,0:T(8,128)S(1)} %fusion.111, f32[128,8192]{1,0:T(8,128)} %get-tuple-element.422, f32[16,8,64,128]{3,2,1,0:T(8,128)} %bitcast.104), kind=kOutput, calls=%fused_computation.8.clone.1 | convolution fusion | flops 1610645504 | bytes 8519684 | tf_op jit(solution)/shard_map/while/body/eval_jaxpr/dot_general | solution.py:30
  321.8 8.3 %fusion.114 = f32[128,1024]{1,0:T(8,128)S(1)} fusion(f32[128,1024]{1,0:T(8,128)S(1)} %get-tuple-element.405, s32[]{:T(128)S(6)} %select_n.64, f32[128,128]{1,0:T(8,128)S(1)} %fusion.113, f32[128,8192]{1,0:T(8,128)S(1)} %copy-done.2, f32[16,8,64,128]{3,2,1,0:T(8,128)} %bitcast.104), kind=kOutput, calls=%fused_computation.11.clone.1 | convolution fusion | flops 1610645504 | bytes 8519684 | tf_op jit(solution)/shard_map/while/body/eval_jaxpr/dot_general | solution.py:30
  330.0 4.8 copy.143
  334.9 96.0 %collective-permute-done.1 = f32[128,72]{1,0:T(8,128)S(1)} collective-permute-done((f32[128,72]{1,0:T(8,128)S(1)}, f32[128,72]{1,0:T(8,128)S(1)}, u32[]{:S(2)}, u32[]{:S(2)}) %collective-permute-start.1) | collective-permute-done | bytes 36896 | tf_op jit(solution)/shard_map/while/body/eval_jaxpr/ppermute | solution.py:26
  431.4 9.2 %fusion.112 = f32[128,1024]{1,0:T(8,128)S(1)} fusion(f32[128,1024]{1,0:T(8,128)S(1)} %get-tuple-element.404, s32[]{:T(128)S(6)} %select_n.64, f32[128,128]{1,0:T(8,128)S(1)} %fusion.111, f32[128,8192]{1,0:T(8,128)} %get-tuple-element.422, f32[16,8,64,128]{3,2,1,0:T(8,128)} %bitcast.104), kind=kOutput, calls=%fused_computation.8.clone.1 | convolution fusion | flops 1610645504 | bytes 8519684 | tf_op jit(solution)/shard_map/while/body/eval_jaxpr/dot_general | solution.py:30
  440.6 8.3 %fusion.114 = f32[128,1024]{1,0:T(8,128)S(1)} fusion(f32[128,1024]{1,0:T(8,128)S(1)} %get-tuple-element.405, s32[]{:T(128)S(6)} %select_n.64, f32[128,128]{1,0:T(8,128)S(1)} %fusion.113, f32[128,8192]{1,0:T(8,128)S(1)} %copy-done.2, f32[16,8,64,128]{3,2,1,0:T(8,128)} %bitcast.104), kind=kOutput, calls=%fused_computation.11.clone.1 | convolution fusion | flops 1610645504 | bytes 8519684 | tf_op jit(solution)/shard_map/while/body/eval_jaxpr/dot_general | solution.py:30
  448.8 4.8 copy.143
  453.6 95.2 %collective-permute-done.1 = f32[128,72]{1,0:T(8,128)S(1)} collective-permute-done((f32[128,72]{1,0:T(8,128)S(1)}, f32[128,72]{1,0:T(8,128)S(1)}, u32[]{:S(2)}, u32[]{:S(2)}) %collective-permute-start.1) | collective-permute-done | bytes 36896 | tf_op jit(solution)/shard_map/while/body/eval_jaxpr/ppermute | solution.py:26
  549.4 9.2 %fusion.112 = f32[128,1024]{1,0:T(8,128)S(1)} fusion(f32[128,1024]{1,0:T(8,128)S(1)} %get-tuple-element.404, s32[]{:T(128)S(6)} %select_n.64, f32[128,128]{1,0:T(8,128)S(1)} %fusion.111, f32[128,8192]{1,0:T(8,128)} %get-tuple-element.422, f32[16,8,64,128]{3,2,1,0:T(8,128)} %bitcast.104), kind=kOutput, calls=%fused_computation.8.clone.1 | convolution fusion | flops 1610645504 | bytes 8519684 | tf_op jit(solution)/shard_map/while/body/eval_jaxpr/dot_general | solution.py:30
  558.6 8.3 %fusion.114 = f32[128,1024]{1,0:T(8,128)S(1)} fusion(f32[128,1024]{1,0:T(8,128)S(1)} %get-tuple-element.405, s32[]{:T(128)S(6)} %select_n.64, f32[128,128]{1,0:T(8,128)S(1)} %fusion.113, f32[128,8192]{1,0:T(8,128)S(1)} %copy-done.2, f32[16,8,64,128]{3,2,1,0:T(8,128)} %bitcast.104), kind=kOutput, calls=%fused_computation.11.clone.1 | convolution fusion | flops 1610645504 | bytes 8519684 | tf_op jit(solution)/shard_map/while/body/eval_jaxpr/dot_general | solution.py:30
  566.9 4.8 copy.143
  573.7 33.8 %all-reduce.3.cloned.1.call-done = (f32[128,8,128]{0,2,1:T(8,128)}, f32[128,8,128]{0,2,1:T(8,128)}) async-done(((f32[128,8,128]{0,2,1:T(8,128)}, f32[128,8,128]{0,2,1:T(8,128)}), (f32[128,8,128]{0,2,1:T(8,128)}, f32[128,8,128]{0,2,1:T(8,128)})) %all-reduce.3.cloned.1.call-update) | async-done | bytes 1048592 | tf_op jit(solution)/shard_map/psum | solution.py:112
  609.6 5.5 all-to-all-start
  617.1 11.9 %all-to-all-done = f32[128,8,128]{2,0,1:T(8,128)S(1)} async-done(((f32[128,8,128]{2,0,1:T(8,128)}), f32[128,8,128]{2,0,1:T(8,128)S(1)}, u32[]{:S(2)}, u32[]{:S(2)}) %all-to-all-start) | async-done | bytes 524320 | tf_op jit(solution)/shard_map/all_to_all | solution.py:116
  629.1 3.6 all-to-all-start.1
  632.7 14.2 %all-to-all-done.1 = f32[128,8,128]{2,0,1:T(8,128)S(1)} async-done(((f32[128,8,128]{2,0,1:T(8,128)}), f32[128,8,128]{2,0,1:T(8,128)S(1)}, u32[]{:S(2)}, u32[]{:S(2)}) %all-to-all-start.1) | async-done | bytes 524320 | tf_op jit(solution)/shard_map/all_to_all | solution.py:117
  (83 shorter events, 23.3 us)
Async XLA Ops:
  7.2 600.3 %all-reduce.3.cloned.1.call-start = ((), (), s32[]{:S(2)}) async-start(), calls=%async_computation.2 | async-start | bytes 2097152 | tf_op jit(solution)/shard_map/psum | solution.py:112
  9.4 9.0 %copy-start = (f32[128,4,16,128]{3,2,1,0:T(8,128)}, f32[128,4,16,128]{3,2,1,0:T(8,128)S(1)}, u32[]{:S(2)}) copy-start(f32[128,4,16,128]{3,2,1,0:T(8,128)S(1)} %copy.150) | copy-start | bytes 12582916
  10.9 58.8 %collective-permute-start.2 = (f32[128,1,16,128]{3,2,1,0:T(8,128)}, f32[128,1,16,128]{3,2,1,0:T(8,128)}, u32[]{:S(2)}, u32[]{:S(2)}) collective-permute-start(f32[128,1,16,128]{3,2,1,0:T(8,128)} %get-tuple-element.320), channel_id=1, source_target_pairs={{1,0},{2,1},{3,2},{0,3},{5,4},{6,5},{7,6},{4,7},{9,8},{10,9},{11,1... | collective-permute-start | bytes 3145736 | tf_op jit(solution)/shard_map/ppermute | solution.py:16
  13.3 56.4 %collective-permute-start.3 = (f32[128,1,16,128]{3,2,1,0:T(8,128)}, f32[128,1,16,128]{3,2,1,0:T(8,128)}, u32[]{:S(2)}, u32[]{:S(2)}) collective-permute-start(f32[128,1,16,128]{3,2,1,0:T(8,128)} %get-tuple-element.321), channel_id=1, source_target_pairs={{0,1},{1,2},{2,3},{3,0},{4,5},{5,6},{6,7},{7,4},{8,9},{9,10},{10,1... | collective-permute-start | bytes 3145736 | tf_op jit(solution)/shard_map/ppermute | solution.py:14
  18.4 20.9 %copy-start.8 = (s32[4]{0:T(128)S(1)}, s32[4]{0:T(128)}, u32[]{:S(2)}) copy-start(s32[4]{0:T(128)} %param.13) | copy-start | bytes 52
  39.2 8.7 %copy-start.5 = (f32[4,18,18]{2,0,1:T(4,128)S(1)}, f32[4,18,18]{2,0,1:T(4,128)}, u32[]{:S(2)}) copy-start(f32[4,18,18]{2,0,1:T(4,128)} %param.11) | copy-start | bytes 15556
  48.9 7.4 %copy-start.6 = (f32[4,18,18]{2,0,1:T(4,128)S(1)}, f32[4,18,18]{2,0,1:T(4,128)}, u32[]{:S(2)}) copy-start(f32[4,18,18]{2,0,1:T(4,128)} %param.12) | copy-start | bytes 15556
  57.2 8.1 %copy-start.1 = (f32[128,4,16,128]{3,2,1,0:T(8,128)S(1)}, f32[128,4,16,128]{3,2,1,0:T(8,128)}, u32[]{:S(2)}) copy-start(f32[128,4,16,128]{3,2,1,0:T(8,128)} %copy-done) | copy-start | bytes 12582916
  65.4 4.3 copy-start.7
  94.9 98.2 %collective-permute-start = (f32[128,4,16,128]{3,2,1,0:T(8,128)}, f32[128,4,16,128]{3,2,1,0:T(8,128)}, u32[]{:S(2)}, u32[]{:S(2)}) collective-permute-start(f32[128,4,16,128]{3,2,1,0:T(8,128)} %get-tuple-element.402), channel_id=1, source_target_pairs={{0,4},{4,8},{8,12},{12,16},{16,20},{20,24},{24,28},{28,0},{1,5},{5... | collective-permute-start | bytes 12582920 | tf_op jit(solution)/shard_map/while/body/eval_jaxpr/ppermute | solution.py:26
  96.4 96.1 %collective-permute-start.1 = (f32[128,72]{1,0:T(8,128)S(1)}, f32[128,72]{1,0:T(8,128)S(1)}, u32[]{:S(2)}, u32[]{:S(2)}) collective-permute-start(f32[128,72]{1,0:T(8,128)S(1)} %get-tuple-element.403), channel_id=1, source_target_pairs={{0,4},{4,8},{8,12},{12,16},{16,20},{20,24},{24,28},{28,0},{1,5},{5... | collective-permute-start | bytes 110600 | tf_op jit(solution)/shard_map/while/body/eval_jaxpr/ppermute | solution.py:26
  193.1 9.2 %copy-start.2 = (f32[128,8192]{1,0:T(8,128)S(1)}, f32[128,8192]{1,0:T(8,128)}, u32[]{:S(2)}) copy-start(f32[128,8192]{1,0:T(8,128)} %get-tuple-element.425) | copy-start | bytes 12582916 | tf_op jit(solution)/shard_map/while
  215.3 97.3 %collective-permute-start = (f32[128,4,16,128]{3,2,1,0:T(8,128)}, f32[128,4,16,128]{3,2,1,0:T(8,128)}, u32[]{:S(2)}, u32[]{:S(2)}) collective-permute-start(f32[128,4,16,128]{3,2,1,0:T(8,128)} %get-tuple-element.402), channel_id=1, source_target_pairs={{0,4},{4,8},{8,12},{12,16},{16,20},{20,24},{24,28},{28,0},{1,5},{5... | collective-permute-start | bytes 12582920 | tf_op jit(solution)/shard_map/while/body/eval_jaxpr/ppermute | solution.py:26
  215.3 96.7 %collective-permute-start.1 = (f32[128,72]{1,0:T(8,128)S(1)}, f32[128,72]{1,0:T(8,128)S(1)}, u32[]{:S(2)}, u32[]{:S(2)}) collective-permute-start(f32[128,72]{1,0:T(8,128)S(1)} %get-tuple-element.403), channel_id=1, source_target_pairs={{0,4},{4,8},{8,12},{12,16},{16,20},{20,24},{24,28},{28,0},{1,5},{5... | collective-permute-start | bytes 110600 | tf_op jit(solution)/shard_map/while/body/eval_jaxpr/ppermute | solution.py:26
  312.6 9.2 %copy-start.2 = (f32[128,8192]{1,0:T(8,128)S(1)}, f32[128,8192]{1,0:T(8,128)}, u32[]{:S(2)}) copy-start(f32[128,8192]{1,0:T(8,128)} %get-tuple-element.425) | copy-start | bytes 12582916 | tf_op jit(solution)/shard_map/while
  334.8 96.5 %collective-permute-start = (f32[128,4,16,128]{3,2,1,0:T(8,128)}, f32[128,4,16,128]{3,2,1,0:T(8,128)}, u32[]{:S(2)}, u32[]{:S(2)}) collective-permute-start(f32[128,4,16,128]{3,2,1,0:T(8,128)} %get-tuple-element.402), channel_id=1, source_target_pairs={{0,4},{4,8},{8,12},{12,16},{16,20},{20,24},{24,28},{28,0},{1,5},{5... | collective-permute-start | bytes 12582920 | tf_op jit(solution)/shard_map/while/body/eval_jaxpr/ppermute | solution.py:26
  334.8 96.0 %collective-permute-start.1 = (f32[128,72]{1,0:T(8,128)S(1)}, f32[128,72]{1,0:T(8,128)S(1)}, u32[]{:S(2)}, u32[]{:S(2)}) collective-permute-start(f32[128,72]{1,0:T(8,128)S(1)} %get-tuple-element.403), channel_id=1, source_target_pairs={{0,4},{4,8},{8,12},{12,16},{16,20},{20,24},{24,28},{28,0},{1,5},{5... | collective-permute-start | bytes 110600 | tf_op jit(solution)/shard_map/while/body/eval_jaxpr/ppermute | solution.py:26
  431.4 9.2 %copy-start.2 = (f32[128,8192]{1,0:T(8,128)S(1)}, f32[128,8192]{1,0:T(8,128)}, u32[]{:S(2)}) copy-start(f32[128,8192]{1,0:T(8,128)} %get-tuple-element.425) | copy-start | bytes 12582916 | tf_op jit(solution)/shard_map/while
  453.6 95.8 %collective-permute-start = (f32[128,4,16,128]{3,2,1,0:T(8,128)}, f32[128,4,16,128]{3,2,1,0:T(8,128)}, u32[]{:S(2)}, u32[]{:S(2)}) collective-permute-start(f32[128,4,16,128]{3,2,1,0:T(8,128)} %get-tuple-element.402), channel_id=1, source_target_pairs={{0,4},{4,8},{8,12},{12,16},{16,20},{20,24},{24,28},{28,0},{1,5},{5... | collective-permute-start | bytes 12582920 | tf_op jit(solution)/shard_map/while/body/eval_jaxpr/ppermute | solution.py:26
  453.6 95.2 %collective-permute-start.1 = (f32[128,72]{1,0:T(8,128)S(1)}, f32[128,72]{1,0:T(8,128)S(1)}, u32[]{:S(2)}, u32[]{:S(2)}) collective-permute-start(f32[128,72]{1,0:T(8,128)S(1)} %get-tuple-element.403), channel_id=1, source_target_pairs={{0,4},{4,8},{8,12},{12,16},{16,20},{20,24},{24,28},{28,0},{1,5},{5... | collective-permute-start | bytes 110600 | tf_op jit(solution)/shard_map/while/body/eval_jaxpr/ppermute | solution.py:26
  549.4 9.2 %copy-start.2 = (f32[128,8192]{1,0:T(8,128)S(1)}, f32[128,8192]{1,0:T(8,128)}, u32[]{:S(2)}) copy-start(f32[128,8192]{1,0:T(8,128)} %get-tuple-element.425) | copy-start | bytes 12582916 | tf_op jit(solution)/shard_map/while
  607.5 39.5 %copy-start.3 = (f32[128,8,128]{0,2,1:T(8,128)S(1)}, f32[128,8,128]{0,2,1:T(8,128)}, u32[]{:S(2)}) copy-start(f32[128,8,128]{0,2,1:T(8,128)} %get-tuple-element.310) | copy-start | bytes 1572868
  607.5 39.5 %copy-start.4 = (f32[128,8,128]{0,2,1:T(8,128)S(1)}, f32[128,8,128]{0,2,1:T(8,128)}, u32[]{:S(2)}) copy-start(f32[128,8,128]{0,2,1:T(8,128)} %get-tuple-element.311) | copy-start | bytes 1572868
  609.6 19.5 %all-to-all-start = ((f32[128,8,128]{2,0,1:T(8,128)}), f32[128,8,128]{2,0,1:T(8,128)S(1)}, u32[]{:S(2)}, u32[]{:S(2)}) async-start(f32[128,8,128]{2,0,1:T(8,128)} %copy.59), calls=%async_computation | async-start | bytes 1048576 | tf_op jit(solution)/shard_map/all_to_all | solution.py:116
  629.1 17.9 %all-to-all-start.1 = ((f32[128,8,128]{2,0,1:T(8,128)}), f32[128,8,128]{2,0,1:T(8,128)S(1)}, u32[]{:S(2)}, u32[]{:S(2)}) async-start(f32[128,8,128]{2,0,1:T(8,128)} %copy.61), calls=%async_computation.1 | async-start | bytes 1048576 | tf_op jit(solution)/shard_map/all_to_all | solution.py:117
Sparse Core Ops, SparseCore 0:
  573.8 33.6 all-reduce.2
where the time goes:
time: 665 us; the launch traced here: 656 us
  waiting for transfers between devices  441 us (66%)
  matrix products  98.1 us (15%)
  local copies, waits for them, and re-layouts  74.6 us (11%)
  starting transfers between devices  15.8 us (2%)
  between operations  14.4 us (2%)
  other arithmetic  11.8 us (2%)
    ppermute x8, waiting for transfers between devices, shifted(): return lax.ppermute(value, axis, pairs)  381 us
    dot_general x21, matrix products, rows_product(): lax.dot_general(left, right, (((1,), (1,)), ((), ())), precision=lax.Prec...  97.6 us
    psum x1, waiting for transfers between devices, on_device(): reduced = lax.psum((summed[0], summed[1]), 'dom')  33.8 us
    while x16, local copies, waits for them, and re-layouts  19.2 us
    unnamed x23, local copies, waits for them, and re-layouts  17.1 us
    all_to_all x1, waiting for transfers between devices, on_device(): lax.all_to_all(ovl_three, 'band', split_axis=1, concat_axis=1, tiled=True)  14.2 us
  transfers between devices with their start and end apart: 13, of which 7 were waited for; matrix products, arithmetic and copies ran while one was open for 9% of the time, Pallas kernels for 0%

commit v1 on v0

v1 whole, which is shorter than its diff:
```python
import functools

import jax
import jax.numpy as jnp
from jax import lax
from jax.experimental import pallas as pl
from jax.experimental.pallas import tpu as pltpu
from jax.sharding import PartitionSpec as P

MESH = pl.DeviceIdType.MESH
CONTRACT_LAST = (((1,), (1,)), ((), ()))


def parts(value):
    high = value.astype(jnp.bfloat16)
    low = (value - high.astype(jnp.float32)).astype(jnp.bfloat16)
    return high, low


def gram_kernel(
    lines, doms, cx, ny, chunks,
    psi, pot, proj, sym, out,
    partner, halo, partner_halo, from_left, from_right, lhs_high, lhs_low,
    left_edges, right_edges, coef, coef_below,
    swap_send, swap_recv, halo_send, halo_recv, fwd_send, fwd_recv,
    right_send, right_recv, left_send, left_recv,
    right_edge_send, right_edge_recv, left_edge_send, left_edge_recv,
    coef_send, coef_recv, pair_send, pair_recv,
):
    rows, bands, nz = psi.shape
    half = rows // 2
    step = half // chunks
    hy = ny // 2
    mine = lax.axis_index("band")
    dom = lax.axis_index("dom")
    line = mine // 2
    side = mine % 2
    mirror = lines - 1 - line
    pair = line * 2 + (1 - side)
    upper = jnp.minimum(line + 1, lines - 1) * 2 + side
    lower = jnp.maximum(line - 1, 0) * 2 + side
    dom_next = (dom + 1) % doms
    dom_prev = (dom + doms - 1) % doms
    ends = lines >= 4

    barrier = pltpu.get_barrier_semaphore()
    pl.semaphore_signal(barrier, inc=1, device_id={"band": pair}, device_id_type=MESH)
    pl.semaphore_signal(barrier, inc=1, device_id={"dom": dom_next}, device_id_type=MESH)
    pl.semaphore_signal(barrier, inc=1, device_id={"dom": dom_prev}, device_id_type=MESH)

    @pl.when(line > 0)
    def _():
        pl.semaphore_signal(barrier, inc=1, device_id={"band": lower}, device_id_type=MESH)

    @pl.when(line < lines - 1)
    def _():
        pl.semaphore_signal(barrier, inc=1, device_id={"band": upper}, device_id_type=MESH)

    peers = 3 + jnp.minimum(line, 1) + jnp.minimum(mirror, 1)
    pl.semaphore_wait(barrier, peers)

    def remote(src, dst, send, recv, where):
        return pltpu.make_async_remote_copy(
            src_ref=src, dst_ref=dst, send_sem=send, recv_sem=recv,
            device_id=where, device_id_type=MESH,
        )

    def seg(ref, at):
        return ref.at[pl.ds(at * hy, hy)]

    segs = 2 * cx
    swaps = [
        remote(seg(psi, at), seg(partner, at), swap_send.at[at], swap_recv.at[at], {"band": pair})
        for at in range(segs)
    ]

    def planes_out(src, dst, send, recv):
        return [
            remote(seg(src, h * cx + at), dst.at[edge, h], send.at[edge, h], recv.at[edge, h], {"dom": to})
            for edge, at, to in ((0, cx - 1, dom_next), (1, 0, dom_prev))
            for h in range(2)
        ]

    halos = planes_out(psi, halo, halo_send, halo_recv)
    forwards = planes_out(partner, partner_halo, fwd_send, fwd_recv)
    coef_swap = remote(coef.at[0], coef.at[1], pair_send.at[0], pair_recv.at[0], {"band": pair})

    def coef_hop(dist):
        src = coef.at[0] if dist == 1 else coef_below.at[dist - 2]
        return remote(src, coef_below.at[dist - 1], coef_send.at[dist - 1], coef_recv.at[dist - 1], {"band": upper})

    ways = (
        (0, half, from_left, right_send, right_recv, upper, line, left_edges, right_edge_send, right_edge_recv),
        (half, 0, from_right, left_send, left_recv, lower, mirror, right_edges, left_edge_send, left_edge_recv),
    )

    def hop(way, dist, chunk, extra=False):
        base, other, slots, send, recv, target = way[:6]
        if extra:
            src = psi.at[pl.ds(other + chunk * step, step)]
        elif dist == 1:
            src = psi.at[pl.ds(base + chunk * step, step)]
        else:
            src = slots.at[dist - 2, pl.ds(chunk * step, step)]
        return remote(
            src, slots.at[dist - 1, pl.ds(chunk * step, step)],
            send.at[dist - 1, chunk], recv.at[dist - 1, chunk], {"band": target},
        )

    def edge_hops(way, dist):
        other, target, slots, send, recv = way[1], way[5], way[7], way[8], way[9]
        return [
            remote(
                psi.at[other + at * hy] if dist == 1 else slots.at[dist - 2, at],
                slots.at[dist - 1, at], send.at[dist - 1, at], recv.at[dist - 1, at], {"band": target},
            )
            for at in range(cx)
        ]

    def sends(way, dist):
        place = way[6]
        go = (place >= dist - 1) & (place < lines - 1)
        if ends and dist == 1:
            go = go & (place != lines - 2)
        return go

    def sends_extra(way):
        return way[6] == 0

    def receives_edges(way, dist):
        place = way[6]
        got = place >= dist
        if ends and dist == 1:
            got = got & (place != lines - 1)
        return got

    def receives(way, dist):
        place = way[6]
        got = receives_edges(way, dist)
        if ends and dist == 2:
            got = got | (place == 1)
        return got

    outer = sorted({0, cx - 1, cx, segs - 1})
    order = outer + [at for at in range(segs) if at not in outer]
    for copy in halos:
        copy.start()
    for chunk in range(chunks):
        for way in ways:
            @pl.when(sends(way, 1))
            def _(way=way, chunk=chunk):
                hop(way, 1, chunk).start()
    for way in ways:
        @pl.when(sends(way, 1))
        def _(way=way):
            for copy in edge_hops(way, 1):
                copy.start()
    for at in order:
        swaps[at].start()
    if ends:
        for chunk in range(chunks):
            for way in ways:
                @pl.when(sends_extra(way))
                def _(way=way, chunk=chunk):
                    hop(way, 2, chunk, True).start()

    def left_operand(src, edges, first):
        for at in range(segs):
            h, plane = at // cx, at % cx
            opposite = (1 - h) * half + plane * hy

            def body(y, carry, at=at, h=h, plane=plane, opposite=opposite):
                r = at * hy + y
                here = src[r]
                before = edges[0, h, y] if plane == 0 else src[r - hy]
                after = edges[1, h, y] if plane == cx - 1 else src[r + hy]
                beside = before + after
                beside = beside + src[jnp.where(y == 0, opposite + hy - 1, r - 1)]
                beside = beside + src[jnp.where(y == hy - 1, opposite, r + 1)]
                beside = beside + pltpu.roll(here, 1, 1) + pltpu.roll(here, nz - 1, 1)
                hpsi = 0.5 * (6.0 * here - beside) + pot[r] * here
                for slot, value in ((first, hpsi), (first + 1, here)):
                    high, low = parts(value)
                    lhs_high[r, pl.ds(slot * bands, bands)] = high
                    lhs_low[r, pl.ds(slot * bands, bands)] = low
                return carry

            lax.fori_loop(0, hy, body, 0)

    def accumulate(group, source, lhs_row, right_row, count):
        where = pl.ds(group * 2 * bands, 2 * bands)

        def body(k, carry):
            left, right = [], []
            for pos in range(2):
                r = lhs_row + 2 * k + pos
                high, low = lhs_high[r, where], lhs_low[r, where]
                other_high, other_low = parts(right_row(2 * k + pos))
                left += [high, high, low]
                right += [other_high, other_low, other_high]
            out[source, where] += lax.dot_general(
                jnp.concatenate(left, axis=1), jnp.concatenate(right, axis=1), CONTRACT_LAST,
                preferred_element_type=jnp.float32,
            )
            return carry

        lax.fori_loop(0, count // 2, body, 0)

    def moved(way, dist, chunk, group):
        base, other, slots, place = way[0], way[1], way[2], way[6]
        rows_at = base
        if ends and dist == 2:
            rows_at = jnp.where(place == 1, other, base)
        accumulate(
            group, source_of(way, dist), rows_at + chunk * step,
            lambda r: slots[dist - 1, chunk * step + r], step,
        )

    def three(left, right):
        left_high, left_low = left
        right_high, right_low = right
        return lax.dot_general(
            jnp.concatenate([left_high, left_high, left_low], axis=1),
            jnp.concatenate([right_high, right_low, right_high], axis=1),
            CONTRACT_LAST, preferred_element_type=jnp.float32,
        )

    def source_of(way, dist):
        from_place = jnp.maximum(way[6] - dist, 0)
        return from_place if way is ways[0] else lines - 1 - from_place

    def fix_edges(way, dist, group):
        base, other, slots, edges = way[0], way[1], way[2], way[7]
        source = source_of(way, dist)
        where = pl.ds((2 * group + 1) * bands, bands)
        into = pl.ds(2 * group * bands, bands)
        for at in range(cx):
            across = other + at * hy + hy - 1
            last = base + at * hy + hy - 1
            out[source, into] += 0.5 * (
                three((lhs_high[across, where], lhs_low[across, where]), parts(slots[dist - 1, at * hy]))
                - three((lhs_high[last, where], lhs_low[last, where]), parts(edges[dist - 1, at]))
            )

    def corrects(way, dist):
        go = receives_edges(way, dist)
        if ends:
            go = go & (way[6] != 1)
        return go

    def project(source, group, right):
        for kind in range(2):
            coupled = lax.dot_general(
                coef[group], sym[kind], (((1,), (0,)), ((), ())),
                precision=lax.Precision.HIGHEST, preferred_element_type=jnp.float32,
            )
            out[source, pl.ds((2 * group + kind) * bands, bands)] += three(parts(coupled), parts(right))

    out[...] = jnp.zeros_like(out)
    coef[0] = jnp.zeros_like(coef[0])
    for copy in halos:
        copy.wait_recv()
    left_operand(psi, halo, 0)

    def coef_body(r, carry):
        own = pl.ds(bands, bands)
        coef[0] += three((lhs_high[r, own], lhs_low[r, own]), parts(proj[r]))
        return carry

    lax.fori_loop(0, rows, coef_body, 0)
    accumulate(0, line, 0, lambda r: psi[r], rows)
    project(line, 0, coef[0])
    coef_swap.start()

    @pl.when(line < lines - 1)
    def _():
        coef_hop(1).start()

    for dist in range(1, lines):
        for chunk in range(chunks):
            for way in ways:
                @pl.when(receives(way, dist))
                def _(way=way, dist=dist, chunk=chunk):
                    hop(way, dist, chunk).wait_recv()

                if dist < lines - 1:
                    @pl.when(sends(way, dist + 1))
                    def _(way=way, dist=dist, chunk=chunk):
                        hop(way, dist + 1, chunk).start()
            for way in ways:
                @pl.when(receives(way, dist))
                def _(way=way, dist=dist, chunk=chunk):
                    moved(way, dist, chunk, 0)
        for way in ways:
            @pl.when(receives_edges(way, dist))
            def _(way=way, dist=dist):
                for copy in edge_hops(way, dist):
                    copy.wait_recv()

            if dist < lines - 1:
                @pl.when(sends(way, dist + 1))
                def _(way=way, dist=dist):
                    for copy in edge_hops(way, dist + 1):
                        copy.start()

            @pl.when(corrects(way, dist))
            def _(way=way, dist=dist):
                fix_edges(way, dist, 0)

        @pl.when(line >= dist)
        def _(dist=dist):
            coef_hop(dist).wait_recv()

        if dist < lines - 1:
            @pl.when((line >= dist) & (line < lines - 1))
            def _(dist=dist):
                coef_hop(dist + 1).start()

        @pl.when(line >= dist)
        def _(dist=dist):
            project(line - dist, 0, coef_below[dist - 1])

        if dist == 1:
            for at in outer:
                swaps[at].wait_recv()
            for copy in forwards:
                copy.start()
    for at in range(segs):
        if at not in outer:
            swaps[at].wait_recv()
    coef_swap.wait_recv()
    for copy in forwards:
        copy.wait_recv()
    left_operand(partner, partner_halo, 2)
    accumulate(1, line, 0, lambda r: psi[r], rows)
    project(line, 1, coef[0])
    for dist in range(1, lines):
        for way in ways:
            @pl.when(receives(way, dist))
            def _(way=way, dist=dist):
                for chunk in range(chunks):
                    moved(way, dist, chunk, 1)

            @pl.when(corrects(way, dist))
            def _(way=way, dist=dist):
                fix_edges(way, dist, 1)

        @pl.when(line >= dist)
        def _(dist=dist):
            project(line - dist, 1, coef_below[dist - 1])

    for copy in swaps + halos + forwards + [coef_swap]:
        copy.wait_send()
    for dist in range(1, lines):
        @pl.when((line >= dist - 1) & (line < lines - 1))
        def _(dist=dist):
            coef_hop(dist).wait_send()

        for way in ways:
            @pl.when(sends(way, dist))
            def _(way=way, dist=dist):
                for copy in edge_hops(way, dist):
                    copy.wait_send()

        for chunk in range(chunks):
            for way in ways:
                go = sends(way, dist)
                if ends and dist == 2:
                    go = go | sends_extra(way)

                @pl.when(go)
                def _(way=way, dist=dist, chunk=chunk):
                    hop(way, dist, chunk).wait_send()


def gram(psi, pot, proj, sym, lines, doms, cx, ny):
    rows, bands, nz = psi.shape
    half = rows // 2
    chunks = 4 if half % 8 == 0 else 1
    hops = lines - 1
    dma = pltpu.SemaphoreType.DMA
    vmem = pl.BlockSpec(memory_space=pltpu.VMEM)
    return pl.pallas_call(
        functools.partial(gram_kernel, lines, doms, cx, ny, chunks),
        out_shape=jax.ShapeDtypeStruct((lines, 4 * bands, bands), jnp.float32),
        in_specs=[vmem] * 4,
        out_specs=vmem,
        scratch_shapes=[
            pltpu.VMEM((rows, bands, nz), jnp.float32),
            pltpu.VMEM((2, 2, ny // 2, bands, nz), jnp.float32),
            pltpu.VMEM((2, 2, ny // 2, bands, nz), jnp.float32),
            pltpu.VMEM((hops, half, bands, nz), jnp.float32),
            pltpu.VMEM((hops, half, bands, nz), jnp.float32),
            pltpu.VMEM((rows, 4 * bands, nz), jnp.bfloat16),
            pltpu.VMEM((rows, 4 * bands, nz), jnp.bfloat16),
            pltpu.VMEM((hops, cx, bands, nz), jnp.float32),
            pltpu.VMEM((hops, cx, bands, nz), jnp.float32),
            pltpu.VMEM((2, bands, proj.shape[1]), jnp.float32),
            pltpu.VMEM((hops, bands, proj.shape[1]), jnp.float32),
            dma((2 * cx,)), dma((2 * cx,)), dma((2, 2)), dma((2, 2)), dma((2, 2)), dma((2, 2)),
            dma((hops, chunks)), dma((hops, chunks)), dma((hops, chunks)), dma((hops, chunks)),
            dma((hops, cx)), dma((hops, cx)), dma((hops, cx)), dma((hops, cx)),
            dma((hops,)), dma((hops,)), dma((1,)), dma((1,)),
        ],
        compiler_params=pltpu.CompilerParams(
            collective_id=0, has_side_effects=True, vmem_limit_bytes=62 * 1024 * 1024
        ),
    )(psi, pot, proj, sym)


def on_device(
    wavefunctions, potential, projectors, hamiltonian_correction, delta_s, projector_count
):
    bands, cx, ny, nz = wavefunctions.shape
    groups = lax.axis_size("band")
    doms = lax.axis_size("dom")
    lines = groups // 2
    mine = lax.axis_index("band")
    line, side = mine // 2, mine % 2
    rows = cx * ny
    volume = 1.0 / (rows * nz * doms)
    hy = ny // 2
    psi = jnp.transpose(wavefunctions.reshape(bands, cx, 2, hy, nz), (2, 1, 3, 0, 4)).reshape(rows, bands, nz)
    pot = jnp.transpose(potential.reshape(cx, 2, hy, nz), (1, 0, 2, 3)).reshape(rows, 1, nz)

    atoms, slots = hamiltonian_correction.shape[:2]
    used = atoms * slots
    width = -(-used // 128) * 128
    mask = (jnp.arange(slots, dtype=jnp.int32)[None, :] < projector_count[:, None]).astype(jnp.float32)
    proj = jnp.transpose(projectors.reshape(used, cx, 2, hy, nz), (2, 1, 3, 0, 4)).reshape(rows, used, nz)
    proj = jnp.pad(proj * mask.reshape(1, used, 1), ((0, 0), (0, width - used), (0, 0)))
    sym = (0.5 / volume) * jnp.stack(
        [
            hamiltonian_correction + jnp.swapaxes(hamiltonian_correction, 1, 2),
            delta_s + jnp.swapaxes(delta_s, 1, 2),
        ]
    )
    same_atom = jnp.eye(atoms, dtype=jnp.float32)[None, :, None, :, None]
    sym = (sym[:, :, :, None, :] * same_atom).reshape(2, used, used)
    sym = jnp.pad(sym, ((0, 0), (0, width - used), (0, width - used)))

    grid = gram(psi, pot, proj, sym, lines, doms, cx, ny)
    here = (jnp.arange(lines, dtype=jnp.int32) == line)[:, None, None, None]
    both = grid.reshape(lines, 4, bands, bands)

    split = 4 % doms == 0
    if split:
        both = lax.all_to_all(both[None], "dom", 2, 0, tiled=True).sum(0)
        first = lax.axis_index("dom") * (4 // doms)
    else:
        both = lax.psum(both, "dom")
        first = 0
    count = both.shape[1]
    lanes = [[at * 2 + s for at in range(lines)] for s in range(2)]
    mirrored = lax.all_to_all(both, "band", 0, 0, axis_index_groups=lanes, tiled=True)
    swapped = lax.ppermute(both, "band", [(i, i ^ 1) for i in range(groups)])
    crossed = ((first + jnp.arange(count, dtype=jnp.int32)) >= 2)[None, :, None, None]
    total = volume * jnp.where(crossed, swapped, both) + volume * jnp.where(here, 0.0, jnp.swapaxes(mirrored, 2, 3))
    if split:
        total = lax.all_gather(total, "dom", axis=1, tiled=True)
    total = total.reshape(lines, 2, 2, bands, bands)
    by_side = jnp.where(side == 0, total, total[:, ::-1])
    final = jnp.transpose(by_side, (2, 3, 0, 1, 4)).reshape(2, bands, groups * bands)
    return final[0], final[1]


def solution(mesh):
    placed = (
        P("band", "dom", None, None),
        P("dom", None, None),
        P("dom", None, None, None, None),
        P("dom", None, None),
        P("dom", None, None),
        P("dom"),
    )
    return jax.shard_map(
        on_device,
        mesh=mesh,
        in_specs=placed,
        out_specs=(P("band", None), P("band", None)),
        check_vma=False,
    )
```

time: 665 us -> 283 us (0.43); the launches traced: 656 us -> 282 us
  waiting for transfers between devices: 441 us -> 23.3 us
  Pallas kernels: 0 us -> 191 us
  matrix products: 98.1 us -> 0 us
  local copies, waits for them, and re-layouts: 74.6 us -> 20.6 us
  blocking collectives: 0 us -> 17.5 us
  other arithmetic: 11.8 us -> 4.43 us
    ppermute x10 -> x1, waiting for transfers between devices: 381 us -> 0.01 us  [on_device(): swapped = lax.ppermute(both, 'band', [(i, i ^ 1) for i in range(groups)])]
    pallas_call x0 -> x1, Pallas kernels: none -> 191 us  [gram(): pl.pallas_call(functools.partial(gram_kernel, lines, doms, cx, ny, chunks...]
    dot_general x23 -> x0, matrix products: 98.1 us -> none  [the longest x21 97.6 us: rows_product(): lax.dot_general(left, right, (((1,), (1,)), ((), ())), precision=lax.Prec...]
    psum x1 -> x0, waiting for transfers between devices: 33.8 us -> none  [on_device(): reduced = lax.psum((summed[0], summed[1]), 'dom')]
    while x21 -> x0, local copies, waits for them, and re-layouts: 21.5 us -> none
    all_to_all x2 -> x1, waiting for transfers between devices: 26.2 us -> 6.97 us  [on_device(): lax.all_to_all(both, 'band', 0, 0, axis_index_groups=lanes, tiled=True)]
    slice x5 -> x3, local copies, waits for them, and re-layouts: 19 us -> 0.46 us  [on_device(): return (final[0], final[1])]
    all_to_all x0 -> x1, blocking collectives: none -> 17.5 us  [on_device(): both = lax.all_to_all(both[None], 'dom', 2, 0, tiled=True).sum(0)]
  transfers between devices with their start and end apart: 13 -> 3, of which waited for: 7 -> 2; matrix products, arithmetic and copies ran while one was open for 9% -> 0% of each run, Pallas kernels for 0% -> 0%
where the time goes in v1:
time: 283 us; the launch traced here: 282 us
  Pallas kernels  191 us (67%)
  waiting for transfers between devices  23.3 us (8%)
  local copies, waits for them, and re-layouts  20.6 us (7%)
  blocking collectives  17.5 us (6%)
  between operations  14.2 us (5%)
  starting transfers between devices  11.5 us (4%)
  other arithmetic  4.43 us (2%)
    pallas_call x1, Pallas kernels, gram(): pl.pallas_call(functools.partial(gram_kernel, lines, doms, cx, ny, chunks...  191 us
    all_to_all x1, blocking collectives, on_device(): both = lax.all_to_all(both[None], 'dom', 2, 0, tiled=True).sum(0)  17.5 us
    all_gather x1, waiting for transfers between devices, on_device(): total = lax.all_gather(total, 'dom', axis=1, tiled=True)  16.4 us
    all_to_all x1, starting transfers between devices, on_device(): lax.all_to_all(both, 'band', 0, 0, axis_index_groups=lanes, tiled=True)  10 us
    all_to_all x1, waiting for transfers between devices, on_device(): lax.all_to_all(both, 'band', 0, 0, axis_index_groups=lanes, tiled=True)  6.97 us
  transfers between devices with their start and end apart: 3, of which 2 were waited for; matrix products, arithmetic and copies ran while one was open for 0% of the time, Pallas kernels for 0%

profile of v1, /device:TPU:0, one launch (start us, length us, event | category | flops | bytes accessed | tf_op | source)
XLA Modules:
  0.0 282.3 jit_solution(5749603718292914076)
XLA Ops:
  7.2 0.7 fusion.4
  7.9 0.1 reshape.97
  8.0 1.4 copy.50
  9.4 0.9 copy.52
  10.2 0.9 copy.53
  11.1 0.8 fusion.2
  12.0 0.1 mul.48
  12.1 0.1 mul.49
  12.3 0.2 mul.47
  12.4 3.0 %copy.51 = f32[72,4,2,8,128]{4,0,3,1,2:T(8,128)S(1)} copy(f32[72,4,2,8,128]{4,3,2,1,0:T(8,128)} %bitcast.43) | data formatting | bytes 4718592 | tf_op jit(solution)/shard_map/reshape | solution.py:430
  15.5 0.7 pad.9.sym
  16.2 0.2 bitcast_multiply_fusion
  16.4 2.7 pad.8.proj
  19.1 1.0 copy-done
  20.1 4.4 %copy.49 = f32[128,4,2,8,128]{4,0,3,1,2:T(8,128)} copy(f32[128,4,2,8,128]{4,3,2,1,0:T(8,128)S(1)} %bitcast.42) | data formatting | bytes 8388608 | tf_op jit(solution)/shard_map/reshape | solution.py:423
  24.5 190.7 %shard_map.77 = f32[4,512,128]{2,1,0:T(8,128)} custom-call(f32[64,128,128]{2,1,0:T(8,128)} %bitcast.39, f32[64,1,128]{2,1,0:T(1,128)} %bitcast.46, f32[64,128,128]{2,1,0:T(8,128)} %pad.8.proj, f32[2,128,128]{2,1,0:T(8,128)} %pad.9.sym), custom_call_target="tpu_custom_call" | custom-call | tf_op jit(solution)/shard_map/pallas_call | solution.py:383
  215.2 1.3 copy.55
  216.5 17.5 %all_to_all.14 = f32[1,4,4,128,128]{4,3,1,0,2:T(8,128)S(1)} all-to-all(f32[1,4,4,128,128]{4,3,1,0,2:T(8,128)S(1)} %copy.55), channel_id=1, replica_groups=mesh['band'=8,'dom'=4] {'dom'}, dimensions={2} | all-to-all | bytes 2097152 | tf_op jit(solution)/shard_map/all_to_all | solution.py:448
  234.0 0.8 reduce_sum.11
  234.8 10.0 %all-to-all-start.1 = ((f32[4,1,128,128]{3,2,1,0:T(8,128)}), f32[4,1,128,128]{3,2,1,0:T(8,128)S(1)}, u32[]{:S(2)}, u32[]{:S(2)}) async-start(f32[4,1,128,128]{3,2,1,0:T(8,128)} %bitcast.15), calls=%async_computation.1 | async-start | bytes 524288 | tf_op jit(solution)/shard_map/all_to_all | solution.py:455
  244.8 1.5 collective-permute-start
  246.3 7.0 %all-to-all-done.1 = f32[4,1,128,128]{3,2,1,0:T(8,128)S(1)} async-done(((f32[4,1,128,128]{3,2,1,0:T(8,128)}), f32[4,1,128,128]{3,2,1,0:T(8,128)S(1)}, u32[]{:S(2)}, u32[]{:S(2)}) %all-to-all-start.1) | async-done | bytes 262176 | tf_op jit(solution)/shard_map/all_to_all | solution.py:455
  253.3 0.1 copy.58
  253.4 1.8 fusion.1
  255.2 16.4 %all-gather.2.cloned.1.call-done = f32[4,4,128,128]{3,2,0,1:T(8,128)} async-done(((f32[4,1,128,128]{3,2,0,1:T(8,128)}), f32[4,4,128,128]{3,2,0,1:T(8,128)}) %all-gather.2.cloned.1.call-update) | async-done | bytes 1048592 | tf_op jit(solution)/shard_map/all_gather | solution.py:460
  271.6 1.3 copy.59
  272.9 0.1 fusion
  273.0 0.1 fusion.6
  273.1 0.2 copy.61
  273.3 1.0 copy.63
  274.3 0.2 copy.60
  274.5 1.0 copy.62
  (10 shorter events, 0.1 us)
Async XLA Ops:
  16.4 3.7 %copy-start = (f32[128,4,16,128]{3,2,1,0:T(8,128)S(1)}, f32[128,4,16,128]{3,2,1,0:T(8,128)}, u32[]{:S(2)}) copy-start(f32[128,4,16,128]{3,2,1,0:T(8,128)} %param.6) | copy-start | bytes 12582916
  234.8 18.5 %all-to-all-start.1 = ((f32[4,1,128,128]{3,2,1,0:T(8,128)}), f32[4,1,128,128]{3,2,1,0:T(8,128)S(1)}, u32[]{:S(2)}, u32[]{:S(2)}) async-start(f32[4,1,128,128]{3,2,1,0:T(8,128)} %bitcast.15), calls=%async_computation.1 | async-start | bytes 524288 | tf_op jit(solution)/shard_map/all_to_all | solution.py:455
  244.8 26.8 %all-gather.2.cloned.1.call-start = ((), (), s32[]{:S(2)}) async-start(), calls=%async_computation.2 | async-start | bytes 1310720 | tf_op jit(solution)/shard_map/all_gather | solution.py:460
  244.8 8.6 %collective-permute-start = (f32[4,1,128,128]{3,2,0,1:T(8,128)}, f32[4,1,128,128]{3,2,0,1:T(8,128)S(1)}, u32[]{:S(2)}, u32[]{:S(2)}) collective-permute-start(f32[4,1,128,128]{3,2,0,1:T(8,128)} %bitcast.14), channel_id=1, source_target_pairs={{0,4},{4,0},{8,12},{12,8},{16,20},{20,16},{24,28},{28,24},{1,5},{5... | collective-permute-start | bytes 786440 | tf_op jit(solution)/shard_map/ppermute | solution.py:456
Sparse Core Ops, SparseCore 0:
  255.4 16.1 all-gather.1
